TPU v7x, 128 devices: a whole 4x4x4 slice. The times are simulated.
128 devices in a mesh: gene: 16 (over z, x), cell: 8 (over y, core).
Axes of the slice: x: 4, y: 4, z: 4, core: 2. Of those that a mesh axis runs over, the one named last changes fastest.
Arguments:
- counts: bfloat16 [32768, 16384], P('gene', 'cell'), may hold values from -6 to 6
- loadings: float32 [32768, 128], P('gene'), may hold values from -0.03125 to 0.03125
- values: float32 [128], replicated, may hold values from 0.5 to 2
- test_matrix: bfloat16 [16384, 128], P('cell'), may hold values from -0.046875 to 0.046875
- tile_mask: int32 [128, 128], P('gene', 'cell'), may hold values 0 or 1
Outputs:
- new_loadings: float32 [32768, 128], P('gene')
- new_values: float32 [128], replicated
All inputs are finite; a program needn't handle non-finite values. No bound on the sum of `tile_mask` on one device may be relied on, other than what follows from the above.
Results may differ from a plain program's by a relative error of at most 0.0028.
Values sent between devices are 32-bit elements; how exact they have to be, the bound alone decides.
A program may use at most 128 MiB of HBM per device.

v0:
```python
import jax
import jax.numpy as jnp
from jax import lax
from jax.sharding import Mesh
from jax.sharding import PartitionSpec as P

GENE_TILE = 256
CELL_TILE = 128
SWEEPS = 3
CELL = ("cell_0", "cell_1")
GENE = ("gene_0", "gene_1")


def in_blocks(array, dim, length):
    before, after = (array.shape[:dim], array.shape[dim + 1 :])
    return jnp.moveaxis(array.reshape(*before, length, -1, *after), dim, 0)


def sent_and_summed(array, axis, dim):
    length = lax.axis_size(axis)
    parts = lax.all_to_all(in_blocks(array, dim, length), axis, 0, 0, tiled=True)
    return jnp.sum(parts, axis=0)


def padded_to(lines, length):
    spare = -lines.shape[0] % length
    if not spare:
        return lines
    return jnp.concatenate([lines, jnp.zeros((spare, *lines.shape[1:]), lines.dtype)])


def copy_for_each(array, axis):
    copies = jnp.broadcast_to(array, (lax.axis_size(axis), *array.shape))
    return lax.all_to_all(copies, axis, split_axis=0, concat_axis=0, tiled=True)


def joined_along(parts, dim):
    parts = jnp.moveaxis(parts, 0, dim)
    shape = parts.shape
    return parts.reshape(*shape[:dim], shape[dim] * shape[dim + 1], *shape[dim + 2 :])


def gather_directly(array, axis, dim):
    parts = copy_for_each(array, axis)
    return joined_along(parts, dim)


def sum_by_parts(array, axes):
    lines = array.reshape(-1, array.shape[-1])
    own = sent_and_summed(padded_to(lines, lax.axis_size(axes)), axes, 0)
    whole = gather_directly(own, axes, 0)
    return whole[: len(lines)].reshape(array.shape)


def total_of_pieces(array, axis):
    return lax.all_gather(array, axis).sum(0)


def sum_by_axis(array, axes, dim):
    far, near = axes
    own = sent_and_summed(in_blocks(array, dim, lax.axis_size(far)), near, dim + 1)
    return jnp.sum(lax.all_to_all(own, far, 0, 0, tiled=True), axis=0)


def gather_axes(array, axes, dim):
    far, near = axes
    leading = copy_for_each(array, far)
    parts = jnp.swapaxes(copy_for_each(leading, near), 0, 1)
    return joined_along(parts.reshape(-1, *array.shape), dim)


def nested_sum(array, axes):
    own = sum_by_axis(padded_to(array, lax.axis_size(axes[0]) * lax.axis_size(axes[1])), axes, 0)
    whole = gather_axes(own, axes, 0)
    return whole[: len(array)].reshape(array.shape)


def in_one(arrays, axis):
    vector, at, finished = (jnp.concatenate([a.reshape(-1) for a in arrays]), 0, [])
    total = nested_sum(vector, axis)
    for a in arrays:
        finished.append(total[at : at + a.size].reshape(a.shape))
        at += a.size
    return tuple(finished)


def contract(left, right):
    return lax.dot_general(
        left,
        right,
        (((0,), (0,)), ((), ())),
        precision=lax.Precision.HIGHEST,
        preferred_element_type=jnp.float32,
    )


def outer_rows(stacked):
    return lax.dot_general(
        stacked,
        stacked,
        (((1,), (1,)), ((), ())),
        precision=lax.Precision.HIGHEST,
        preferred_element_type=jnp.float32,
    )


def local(counts, loadings, values, test_matrix, tile_mask):
    highest = lax.Precision.HIGHEST
    gene_rows, cell_cols = counts.shape
    components = loadings.shape[1]
    sketch_width = test_matrix.shape[1]
    cells_total = cell_cols * lax.axis_size(CELL)
    genes_total = gene_rows * lax.axis_size(GENE)
    tile_wide = jnp.repeat(
        jnp.repeat(tile_mask.astype(jnp.bfloat16), GENE_TILE, axis=0), CELL_TILE, axis=1
    )
    masked = counts * tile_wide
    load_narrow = loadings.astype(jnp.bfloat16)
    proj_part = lax.dot_general(
        load_narrow, masked, (((0,), (0,)), ((), ())), preferred_element_type=jnp.float32
    )
    projection = sum_by_parts(proj_part, GENE)
    test_wide = test_matrix.astype(jnp.float32)
    raw_part = jnp.dot(masked, test_matrix, preferred_element_type=jnp.float32)
    small_part = jnp.dot(projection, test_wide, precision=highest)
    raw_sketch, small_sketch = (total_of_pieces(raw_part, CELL), total_of_pieces(small_part, CELL))
    sketch = raw_sketch - jnp.dot(loadings, small_sketch, precision=highest)
    rows_left = sketch.T
    along_loadings = jnp.dot(rows_left, loadings, precision=highest)
    inner = sent_and_summed(
        jnp.dot(rows_left, masked, precision=highest, preferred_element_type=jnp.float32)
        - jnp.dot(along_loadings, projection, precision=highest),
        GENE,
        1,
    )
    share_width = inner.shape[1]
    offset = lax.axis_index(GENE) * share_width
    proj_share = lax.dynamic_slice_in_dim(projection, offset, share_width, 1)
    test_share = lax.dynamic_slice_in_dim(test_wide, offset, share_width, 0)
    stacked = jnp.concatenate([proj_share, inner], axis=0)
    gram_part = jnp.dot(inner, test_share, precision=highest)
    core_raw, sketch_gram = in_one(
        (outer_rows(stacked), gram_part), (("gene_0", "gene_1", "cell_0"), "cell_1")
    )
    factor = jnp.linalg.cholesky(sketch_gram)
    basis_rows = jax.scipy.linalg.solve_triangular(factor, sketch.T, lower=True)
    factor_inverse = jax.scipy.linalg.solve_triangular(
        factor, jnp.eye(sketch_width, dtype=jnp.float32), lower=True
    )
    transform = jnp.zeros((components + sketch_width, components + sketch_width), jnp.float32)
    transform = transform.at[:components, :components].set(jnp.eye(components, dtype=jnp.float32))
    transform = transform.at[components:, components:].set(factor_inverse)
    core_sum = jnp.dot(
        jnp.dot(transform, core_raw, precision=highest), transform.T, precision=highest
    )
    squares = jnp.concatenate([values * values, jnp.zeros((sketch_width,), jnp.float32)])
    core_matrix = core_sum / cells_total + jnp.diag(squares)
    subspace = jnp.eye(components + sketch_width, components, dtype=jnp.float32)
    for sweep in range(SWEEPS):
        image_block = jnp.dot(core_matrix, subspace, precision=highest)
        chol = jnp.linalg.cholesky(contract(image_block, image_block))
        subspace = jax.scipy.linalg.solve_triangular(chol, image_block.T, lower=True).T
    final_image = jnp.dot(core_matrix, subspace, precision=highest)
    new_values = jnp.sqrt(jnp.sum(subspace * final_image, axis=0))
    rotated = jnp.dot(loadings, subspace[:components], precision=highest) + contract(
        basis_rows, subspace[components:]
    )
    new_loadings = rotated * genes_total**0.5
    return (new_loadings, new_values)


def solution(mesh):
    torus = Mesh(mesh.devices.reshape(4, 4, 4, 2), ("gene_0", "gene_1", "cell_0", "cell_1"))
    placed = (P(GENE, CELL), P(GENE, None), P(), P(CELL, None), P(GENE, CELL))
    return jax.shard_map(
        local, mesh=torus, in_specs=placed, out_specs=(P(GENE, None), P()), check_vma=False
    )
```

profile of v0, /device:TPU:1, one launch (start us, length us, event | category | flops | bytes accessed | tf_op | source)
XLA Modules:
  0.0 294.2 jit_solution(12753913997079958920)
XLA Ops:
  8.2 9.0 %broadcast_in_dim.37 = bf16[2048,16,128]{2,1,0:T(8,128)(2,1)S(1)} broadcast(bf16[2048,16]{1,0:T(8,128)(2,1)S(1)} %bitcast.129), dimensions={0,1} | broadcast | bytes 8454144 | tf_op jit(solution)/shard_map/broadcast_in_dim | solution.py:114
  17.1 3.2 %copy-done.4 = bf16[2048,16,128]{2,1,0:T(8,128)(2,1)} copy-done((bf16[2048,16,128]{2,1,0:T(8,128)(2,1)}, bf16[2048,16,128]{2,1,0:T(8,128)(2,1)S(1)}, u32[]{:S(2)}) %copy-start.4) | copy-done | bytes 8388632
  20.4 3.7 %fusion.49 = f32[2048,128]{1,0:T(8,128)} fusion(bf16[2048,128]{1,0:T(8,128)(2,1)S(1)} %copy-done, bf16[2048,2048]{1,0:T(8,128)(2,1)S(1)} %copy-done.5, bf16[256,8,16,128]{3,2,1,0:T(8,128)(2,1)S(1)} %bitcast.125), kind=kOutput, calls=%fused_computation.81 | convolution fusion | flops 1077936128 | bytes 18350080 | tf_op jit(solution)/shard_map/dot_general | solution.py:124
  24.1 7.4 %convolution_bitcast_fusion = f32[16,8,2048]{2,1,0:T(8,128)S(1)} fusion(f32[2048,128]{1,0:T(8,128)S(1)} %copy-done.1, bf16[2048,2048]{1,0:T(8,128)(2,1)} %param.12, bf16[256,8,16,128]{3,2,1,0:T(8,128)(2,1)} %bitcast.126), kind=kOutput, calls=%fused_computation.1 | convolution fusion | flops 1078198272 | bytes 18874368 | tf_op jit(solution)/shard_map/dot_general | solution.py:119
  31.5 24.3 %all_to_all.43 = f32[16,8,2048]{2,1,0:T(8,128)S(1)} all-to-all(f32[16,8,2048]{2,1,0:T(8,128)S(1)} %convolution_bitcast_fusion), channel_id=1, replica_groups=mesh['gene_0'=4,'gene_1'=4,'cell_0'=4,'cell_1'=2] {'gene_0','gene_1'}, dimensions={0} | all-to-all | bytes 2097152 | tf_op jit(solution)/shard_map/all_to_all | solution.py:21
  55.9 19.1 %all_to_all.44 = f32[16,8,2048]{2,1,0:T(8,128)S(1)} all-to-all(f32[16,8,2048]{2,1,0:T(8,128)S(1)} %broadcast_in_dim.38), channel_id=1, replica_groups=mesh['gene_0'=4,'gene_1'=4,'cell_0'=4,'cell_1'=2] {'gene_0','gene_1'}, dimensions={0} | all-to-all | bytes 2097152 | tf_op jit(solution)/shard_map/all_to_all | solution.py:34
  75.7 16.2 %all-gather.1 = f32[1024,128]{1,0:T(8,128)S(1)} all-gather(f32[128,128]{1,0:T(8,128)S(1)} %fusion.46), channel_id=3, replica_groups=mesh['gene_0'=4,'gene_1'=4,'cell_0'=4,'cell_1'=2] {'cell_0','cell_1'}, dimensions={0}, use_global_device_ids=true | all-gather | bytes 589824 | tf_op jit(solution)/shard_map/all_gather | solution.py:56
  92.0 4.9 %reduce_sum.64 = f32[2048,128]{1,0:T(8,128)} reduce(f32[8,2048,128]{2,1,0:T(8,128)} %bitcast.124, f32[]{:T(128)} %constant.115.clone.1), dimensions={0}, to_apply=%region_1.0 | reduce | flops 1835008 | bytes 9437188 | tf_op jit(solution)/shard_map/reduce_sum | solution.py:56
  96.9 2.6 copy.34
  99.5 2.3 fusion
  101.9 9.0 %fusion.48 = f32[128,2048]{1,0:T(8,128)S(1)} fusion(f32[2048,128]{0,1:T(8,128)S(1)} %fusion, bf16[2048,2048]{1,0:T(8,128)(2,1)} %param.12, bf16[256,8,16,128]{3,2,1,0:T(8,128)(2,1)} %bitcast.127), kind=kOutput, calls=%fused_computation.80 | convolution fusion | flops 6446645248 | bytes 18874368 | tf_op jit(solution)/shard_map/dot_general | solution.py:131
  110.9 1.2 fusion.50
  113.1 1.1 copy.60
  114.3 4.3 %all-to-all-start.2 = ((f32[16,128,128]{2,1,0:T(8,128)}), f32[16,128,128]{2,1,0:T(8,128)}, u32[]{:S(2)}, u32[]{:S(2)}) async-start(f32[16,128,128]{2,1,0:T(8,128)} %bitcast.128), calls=%async_computation.2 | async-start | bytes 2097152 | tf_op jit(solution)/shard_map/all_to_all | solution.py:21
  118.6 18.2 %all-to-all-done.2 = f32[16,128,128]{2,1,0:T(8,128)} async-done(((f32[16,128,128]{2,1,0:T(8,128)}), f32[16,128,128]{2,1,0:T(8,128)}, u32[]{:S(2)}, u32[]{:S(2)}) %all-to-all-start.2) | async-done | bytes 1048608 | tf_op jit(solution)/shard_map/all_to_all | solution.py:21
  136.8 1.3 reduce_sum.66
  139.1 4.6 %all_to_all.45 = f32[2,64,640]{2,1,0:T(8,128)S(1)} all-to-all(f32[2,64,640]{2,1,0:T(8,128)S(1)} %copy.36), channel_id=1, replica_groups=mesh['gene_0'=4,'gene_1'=4,'cell_0'=4,'cell_1'=2] {'cell_1'}, dimensions={0} | all-to-all | bytes 655360 | tf_op jit(solution)/shard_map/all_to_all | solution.py:21
  143.9 14.2 %all_to_all.46 = f32[64,1,640]{2,1,0:T(1,128)S(1)} all-to-all(f32[64,1,640]{2,1,0:T(1,128)S(1)} %all_to_all.31), channel_id=1, replica_groups=mesh['gene_0'=4,'gene_1'=4,'cell_0'=4,'cell_1'=2] {'gene_0','gene_1','ce..., dimensions={0} | all-to-all | bytes 327680 | tf_op jit(solution)/shard_map/all_to_all | solution.py:62
  159.0 4.9 %all-to-all-start.5 = ((f32[64,1,640]{2,1,0:T(1,128)}), f32[64,1,640]{2,1,0:T(1,128)S(1)}, u32[]{:S(2)}, u32[]{:S(2)}) async-start(f32[64,1,640]{2,1,0:T(1,128)} %broadcast_in_dim.39), calls=%async_computation.5 | async-start | bytes 327680 | tf_op jit(solution)/shard_map/all_to_all | solution.py:34
  164.0 8.8 %all-to-all-done.5 = f32[64,1,640]{2,1,0:T(1,128)S(1)} async-done(((f32[64,1,640]{2,1,0:T(1,128)}), f32[64,1,640]{2,1,0:T(1,128)S(1)}, u32[]{:S(2)}, u32[]{:S(2)}) %all-to-all-start.5) | async-done | bytes 163872 | tf_op jit(solution)/shard_map/all_to_all | solution.py:34
  172.9 6.6 %all_to_all.47 = f32[2,64,640]{2,1,0:T(8,128)S(1)} all-to-all(f32[2,64,640]{2,1,0:T(8,128)S(1)} %broadcast_in_dim.40), channel_id=1, replica_groups=mesh['gene_0'=4,'gene_1'=4,'cell_0'=4,'cell_1'=2] {'cell_1'}, dimensions={0} | all-to-all | bytes 655360 | tf_op jit(solution)/shard_map/all_to_all | solution.py:34
  182.7 11.7 %cholesky.74 = f32[128,128]{1,0:T(8,128)S(1)} custom-call(f32[128,128]{1,0:T(8,128)S(1)} %fusion.35), custom_call_target="Cholesky" | custom-call | tf_op jit(solution)/shard_map/jit(cholesky)/cholesky | solution.py:145
  195.8 9.8 %custom-call.12 = f32[1,128,128]{1,2,0:T(8,128)S(1)} custom-call(f32[1,128,128]{2,1,0:T(8,128)S(1)} %fusion.19), custom_call_target="InvertDiagBlocksLowerTriangular" | custom-call | tf_op jit(solution)/shard_map/jit(_solve_triangular)/triangular_solve | solution.py:147
  205.6 2.0 fusion.32
  209.5 11.9 %cholesky.85 = f32[128,128]{1,0:T(8,128)S(1)} custom-call(f32[128,128]{1,0:T(8,128)S(1)} %fusion.31), custom_call_target="Cholesky" | custom-call | tf_op jit(solution)/shard_map/jit(cholesky)/cholesky | solution.py:161
  222.7 9.8 %custom-call.15 = f32[1,128,128]{1,2,0:T(8,128)S(1)} custom-call(f32[1,128,128]{2,1,0:T(8,128)S(1)} %fusion.20), custom_call_target="InvertDiagBlocksLowerTriangular" | custom-call | tf_op jit(solution)/shard_map/jit(_solve_triangular)/triangular_solve | solution.py:162
  233.7 11.7 %cholesky.96 = f32[128,128]{1,0:T(8,128)S(1)} custom-call(f32[128,128]{1,0:T(8,128)S(1)} %fusion.29), custom_call_target="Cholesky" | custom-call | tf_op jit(solution)/shard_map/jit(cholesky)/cholesky | solution.py:161
  246.8 9.8 %custom-call.16 = f32[1,128,128]{1,2,0:T(8,128)S(1)} custom-call(f32[1,128,128]{2,1,0:T(8,128)S(1)} %fusion.21), custom_call_target="InvertDiagBlocksLowerTriangular" | custom-call | tf_op jit(solution)/shard_map/jit(_solve_triangular)/triangular_solve | solution.py:162
  257.8 11.9 %cholesky.107 = f32[128,128]{1,0:T(8,128)S(1)} custom-call(f32[128,128]{1,0:T(8,128)S(1)} %fusion.27), custom_call_target="Cholesky" | custom-call | tf_op jit(solution)/shard_map/jit(cholesky)/cholesky | solution.py:161
  271.1 9.8 %custom-call.17 = f32[1,128,128]{1,2,0:T(8,128)S(1)} custom-call(f32[1,128,128]{2,1,0:T(8,128)S(1)} %fusion.22), custom_call_target="InvertDiagBlocksLowerTriangular" | custom-call | tf_op jit(solution)/shard_map/jit(_solve_triangular)/triangular_solve | solution.py:162
  281.7 2.3 fusion.23
  285.1 1.3 copy.46
  (79 shorter events, 20.0 us)
Async XLA Ops:
  7.2 13.2 %copy-start = (bf16[2048,128]{1,0:T(8,128)(2,1)S(1)}, bf16[2048,128]{1,0:T(8,128)(2,1)}, u32[]{:S(2)}) copy-start(bf16[2048,128]{1,0:T(8,128)(2,1)} %param.15) | copy-start | bytes 1572868
  7.2 84.8 %all-gather.4.cloned.1.call-start = ((), (), s32[]{:S(2)}) async-start(), calls=%async_computation.7 | async-start | bytes 9437184 | tf_op jit(solution)/shard_map/all_gather | solution.py:56
  7.2 13.1 %copy-start.5 = (bf16[2048,2048]{1,0:T(8,128)(2,1)S(1)}, bf16[2048,2048]{1,0:T(8,128)(2,1)}, u32[]{:S(2)}) copy-start(bf16[2048,2048]{1,0:T(8,128)(2,1)} %param.12) | copy-start | bytes 25165828
  17.1 3.2 %copy-start.4 = (bf16[2048,16,128]{2,1,0:T(8,128)(2,1)}, bf16[2048,16,128]{2,1,0:T(8,128)(2,1)S(1)}, u32[]{:S(2)}) copy-start(bf16[2048,16,128]{2,1,0:T(8,128)(2,1)S(1)} %broadcast_in_dim.37) | copy-start | bytes 25165828
  20.4 3.7 %copy-start.1 = (f32[2048,128]{1,0:T(8,128)S(1)}, f32[2048,128]{1,0:T(8,128)}, u32[]{:S(2)}) copy-start(f32[2048,128]{1,0:T(8,128)} %param.13) | copy-start | bytes 3145732
  101.8 9.1 %copy-start.2 = (f32[2048,128]{0,1:T(8,128)}, f32[2048,128]{0,1:T(8,128)S(1)}, u32[]{:S(2)}) copy-start(f32[2048,128]{0,1:T(8,128)S(1)} %fusion) | copy-start | bytes 3145732
  110.9 53.0 %copy-start.6 = (f32[128]{0:T(128)S(1)}, f32[128]{0:T(128)}, u32[]{:S(2)}) copy-start(f32[128]{0:T(128)} %param.14) | copy-start | bytes 1540
  114.3 22.6 %all-to-all-start.2 = ((f32[16,128,128]{2,1,0:T(8,128)}), f32[16,128,128]{2,1,0:T(8,128)}, u32[]{:S(2)}, u32[]{:S(2)}) async-start(f32[16,128,128]{2,1,0:T(8,128)} %bitcast.128), calls=%async_computation.2 | async-start | bytes 2097152 | tf_op jit(solution)/shard_map/all_to_all | solution.py:21
  118.6 87.0 %copy-start.3 = (f32[2048,128]{0,1:T(8,128)S(1)}, f32[2048,128]{0,1:T(8,128)}, u32[]{:S(2)}) copy-start(f32[2048,128]{0,1:T(8,128)} %copy-done.2) | copy-start | bytes 3145732
  159.0 13.9 %all-to-all-start.5 = ((f32[64,1,640]{2,1,0:T(1,128)}), f32[64,1,640]{2,1,0:T(1,128)S(1)}, u32[]{:S(2)}, u32[]{:S(2)}) async-start(f32[64,1,640]{2,1,0:T(1,128)} %broadcast_in_dim.39), calls=%async_computation.5 | async-start | bytes 327680 | tf_op jit(solution)/shard_map/all_to_all | solution.py:34
Sparse Core Ops, SparseCore 0:
  24.2 53.2 all-gather.3
where the time goes:
time: 300 us; the launch traced here: 294 us
  other arithmetic  100 us (33%)
  blocking collectives  85.1 us (28%)
  matrix products  35.8 us (12%)
  waiting for transfers between devices  27.1 us (9%)
  local copies, waits for them, and re-layouts  21.9 us (7%)
  between operations  15 us (5%)
  starting transfers between devices  9.31 us (3%)
    another operation x10, other arithmetic, local(): chol = jnp.linalg.cholesky(contract(image_block, image_block))  37.6 us
    another operation x6, other arithmetic, local(): jax.scipy.linalg.solve_triangular(chol, image_block.T, lower=True)  31.4 us
    all_to_all x2, blocking collectives, sent_and_summed(): lax.all_to_all(in_blocks(array, dim, length), axis, 0, 0, tiled=True)  28.9 us
    all_to_all x2, blocking collectives, copy_for_each(): return lax.all_to_all(copies, axis, split_axis=0, concat_axis=0, tiled=True)  25.7 us
    all_to_all x1, waiting for transfers between devices, sent_and_summed(): lax.all_to_all(in_blocks(array, dim, length), axis, 0, 0, tiled=True)  18.2 us
    all_gather x1, blocking collectives, total_of_pieces(): return lax.all_gather(array, axis).sum(0)  16.2 us
    all_to_all x1, blocking collectives, sum_by_axis(): return jnp.sum(lax.all_to_all(own, far, 0, 0, tiled=True), axis=0)  14.2 us
    another operation x3, other arithmetic, local(): factor = jnp.linalg.cholesky(sketch_gram)  12.4 us
  transfers between devices with their start and end apart: 3, of which 2 were waited for; matrix products, arithmetic and copies ran while one was open for 3% of the time, Pallas kernels for 0%

commit v1 on v0

--- a/solution.py
+++ b/solution.py
@@ -1,12 +1,16 @@
+import functools
 import jax
 import jax.numpy as jnp
 from jax import lax
+from jax.experimental import pallas as pl
+from jax.experimental.pallas import tpu as pltpu
 from jax.sharding import Mesh
 from jax.sharding import PartitionSpec as P
 
 GENE_TILE = 256
 CELL_TILE = 128
 SWEEPS = 3
+BLOCK = 32
 CELL = ("cell_0", "cell_1")
 GENE = ("gene_0", "gene_1")
 
@@ -102,6 +106,100 @@
         precision=lax.Precision.HIGHEST,
         preferred_element_type=jnp.float32,
     )
+
+
+def dot(left, right, left_dim, right_dim):
+    return lax.dot_general(
+        left,
+        right,
+        (((left_dim,), (right_dim,)), ((), ())),
+        precision=lax.Precision.HIGHEST,
+        preferred_element_type=jnp.float32,
+    )
+
+
+def identity(size):
+    row = lax.broadcasted_iota(jnp.int32, (size, size), 0)
+    column = lax.broadcasted_iota(jnp.int32, (size, size), 1)
+    return jnp.where(row == column, 1.0, 0.0).astype(jnp.float32)
+
+
+def inverse_factor(work, gram):
+    size = gram.shape[0]
+    work[:, :size] = gram
+    work[:, size:] = identity(size)
+    row_of = lax.broadcasted_iota(jnp.int32, (BLOCK, size), 0)
+    for start in range(0, size, BLOCK):
+        panel = work[start : start + BLOCK, :]
+        columns = [
+            jnp.broadcast_to(panel[:, start + j : start + j + 1], (BLOCK, size))
+            for j in range(BLOCK)
+        ]
+        halves = [panel[:, :size], panel[:, size:]]
+        pivots = jnp.zeros((BLOCK, size), jnp.float32)
+        for j in range(BLOCK):
+            column = columns[j]
+            spread = jnp.broadcast_to(column[j : j + 1], (BLOCK, size))
+            inverse = 1.0 / spread
+            pivots = jnp.where(row_of == j, spread, pivots)
+            for k in range(j + 1, BLOCK):
+                lead = jnp.broadcast_to(column[k : k + 1], (BLOCK, size))
+                columns[k] = columns[k] - column * (lead * inverse)
+            ratio = jnp.where(row_of > j, column * inverse, 0.0)
+            halves = [h - ratio * jnp.broadcast_to(h[j : j + 1], (BLOCK, size)) for h in halves]
+        scale = lax.rsqrt(pivots)
+        panel = jnp.concatenate([h * scale for h in halves], axis=1)
+        work[start : start + BLOCK, :] = panel
+        if start + BLOCK < size:
+            update = dot(panel[:, :size], panel, 0, 0)
+            work[start + BLOCK :, :] = work[start + BLOCK :, :] - update[start + BLOCK :, :]
+    return work[:, size:]
+
+
+def subspace_kernel(
+    cells_total, core_ref, gram_ref, values_ref, top_ref, bottom_ref, squares_ref, work, core, subspace, basis
+):
+    size = gram_ref.shape[0]
+    basis[...] = inverse_factor(work, gram_ref[...])
+    inverse = basis[...]
+    values = values_ref[...]
+    cross = dot(inverse, core_ref[size:, :size], 1, 0)
+    corner = dot(dot(inverse, core_ref[size:, size:], 1, 0), inverse, 1, 1)
+    squares = jnp.broadcast_to(values * values, (size, size)) * identity(size)
+    core[:size, :size] = core_ref[:size, :size] / cells_total + squares
+    core[size:, :size] = cross / cells_total
+    core[:size, size:] = dot(core_ref[:size, size:], inverse, 1, 1) / cells_total
+    core[size:, size:] = corner / cells_total
+    subspace[:size] = identity(size)
+    subspace[size:] = jnp.zeros((size, size), jnp.float32)
+
+    def sweep(step, carry):
+        image = dot(core[...], subspace[...], 1, 0)
+        rotation = inverse_factor(work, dot(image, image, 0, 0))
+        subspace[...] = dot(image, rotation, 1, 1)
+        return carry
+
+    lax.fori_loop(0, SWEEPS, sweep, 0)
+    final = dot(core[...], subspace[...], 1, 0)
+    squares_ref[...] = jnp.sum(subspace[...] * final, axis=0, keepdims=True)
+    top_ref[...] = subspace[:size]
+    bottom_ref[...] = dot(basis[...], subspace[size:], 0, 0)
+
+
+def subspace_call(core_raw, gram, values, cells_total):
+    size = gram.shape[0]
+    shape = lambda *dims: jax.ShapeDtypeStruct(dims, jnp.float32)
+    return pl.pallas_call(
+        functools.partial(subspace_kernel, cells_total),
+        out_shape=(shape(size, size), shape(size, size), shape(1, size)),
+        scratch_shapes=[
+            pltpu.VMEM((size, 2 * size), jnp.float32),
+            pltpu.VMEM((2 * size, 2 * size), jnp.float32),
+            pltpu.VMEM((2 * size, size), jnp.float32),
+            pltpu.VMEM((size, size), jnp.float32),
+        ],
+        name="subspace",
+    )(core_raw, gram, values.reshape(1, size))
 
 
 def local(counts, loadings, values, test_matrix, tile_mask):
@@ -142,31 +240,12 @@
     core_raw, sketch_gram = in_one(
         (outer_rows(stacked), gram_part), (("gene_0", "gene_1", "cell_0"), "cell_1")
     )
-    factor = jnp.linalg.cholesky(sketch_gram)
-    basis_rows = jax.scipy.linalg.solve_triangular(factor, sketch.T, lower=True)
-    factor_inverse = jax.scipy.linalg.solve_triangular(
-        factor, jnp.eye(sketch_width, dtype=jnp.float32), lower=True
-    )
-    transform = jnp.zeros((components + sketch_width, components + sketch_width), jnp.float32)
-    transform = transform.at[:components, :components].set(jnp.eye(components, dtype=jnp.float32))
-    transform = transform.at[components:, components:].set(factor_inverse)
-    core_sum = jnp.dot(
-        jnp.dot(transform, core_raw, precision=highest), transform.T, precision=highest
-    )
-    squares = jnp.concatenate([values * values, jnp.zeros((sketch_width,), jnp.float32)])
-    core_matrix = core_sum / cells_total + jnp.diag(squares)
-    subspace = jnp.eye(components + sketch_width, components, dtype=jnp.float32)
-    for sweep in range(SWEEPS):
-        image_block = jnp.dot(core_matrix, subspace, precision=highest)
-        chol = jnp.linalg.cholesky(contract(image_block, image_block))
-        subspace = jax.scipy.linalg.solve_triangular(chol, image_block.T, lower=True).T
-    final_image = jnp.dot(core_matrix, subspace, precision=highest)
-    new_values = jnp.sqrt(jnp.sum(subspace * final_image, axis=0))
-    rotated = jnp.dot(loadings, subspace[:components], precision=highest) + contract(
-        basis_rows, subspace[components:]
+    top, bottom, squares_out = subspace_call(core_raw, sketch_gram, values, cells_total)
+    rotated = jnp.dot(loadings, top, precision=highest) + jnp.dot(
+        sketch, bottom, precision=highest
     )
     new_loadings = rotated * genes_total**0.5
-    return (new_loadings, new_values)
+    return (new_loadings, jnp.sqrt(squares_out[0]))
 
 
 def solution(mesh):

time: 300 us -> 217 us (0.72); the launches traced: 294 us -> 216 us
  other arithmetic: 100 us -> 7.25 us
  Pallas kernels: 0 us -> 20.9 us
  blocking collectives: 85.1 us -> 98.6 us
  waiting for transfers between devices: 27.1 us -> 18.2 us
  matrix products: 35.8 us -> 29.7 us
  starting transfers between devices: 9.31 us -> 4.37 us
    another operation x21 -> x0, other arithmetic: 91.8 us -> none  [the longest x10 37.6 us: local(): chol = jnp.linalg.cholesky(contract(image_block, image_block))]
    pallas_call x0 -> x1, Pallas kernels: none -> 20.9 us  [subspace_call(): pl.pallas_call(functools.partial(subspace_kernel, cells_total), out_shape...]
    all_to_all x2 -> x3, blocking collectives: 25.7 us -> 39.5 us  [copy_for_each(): return lax.all_to_all(copies, axis, split_axis=0, concat_axis=0, tiled=True)]
    all_to_all x1 -> x0, waiting for transfers between devices: 8.85 us -> none  [copy_for_each(): return lax.all_to_all(copies, axis, split_axis=0, concat_axis=0, tiled=True)]
    all_to_all x1 -> x0, starting transfers between devices: 4.94 us -> none  [copy_for_each(): return lax.all_to_all(copies, axis, split_axis=0, concat_axis=0, tiled=True)]
    another operation x5 -> x0, matrix products: 3.21 us -> none  [the longest x1 2.03 us: local(): basis_rows = jax.scipy.linalg.solve_triangular(factor, sketch.T, lower=True)]
    dot_general x11 -> x2, matrix products: 6.78 us -> 3.84 us  [the longest x1 1.92 us: local(): jnp.dot(loadings, top, precision=highest)]
  transfers between devices with their start and end apart: 3 -> 2, of which waited for: 2 -> 1; matrix products, arithmetic and copies ran while one was open for 3% -> 4% of each run, Pallas kernels for 0% -> 0%
where the time goes in v1:
time: 217 us; the launch traced here: 216 us
  blocking collectives  98.6 us (45%)
  matrix products  29.7 us (14%)
  local copies, waits for them, and re-layouts  22.8 us (11%)
  Pallas kernels  20.9 us (10%)
  waiting for transfers between devices  18.2 us (8%)
  between operations  14.3 us (7%)
  other arithmetic  7.25 us (3%)
  starting transfers between devices  4.37 us (2%)
    all_to_all x3, blocking collectives, copy_for_each(): return lax.all_to_all(copies, axis, split_axis=0, concat_axis=0, tiled=True)  39.5 us
    all_to_all x2, blocking collectives, sent_and_summed(): lax.all_to_all(in_blocks(array, dim, length), axis, 0, 0, tiled=True)  28.9 us
    pallas_call x1, Pallas kernels, subspace_call(): pl.pallas_call(functools.partial(subspace_kernel, cells_total), out_shape...  20.9 us
    all_to_all x1, waiting for transfers between devices, sent_and_summed(): lax.all_to_all(in_blocks(array, dim, length), axis, 0, 0, tiled=True)  18.2 us
    all_gather x1, blocking collectives, total_of_pieces(): return lax.all_gather(array, axis).sum(0)  16 us
    all_to_all x1, blocking collectives, sum_by_axis(): return jnp.sum(lax.all_to_all(own, far, 0, 0, tiled=True), axis=0)  14.2 us
    dot_general x1, matrix products, local(): jnp.dot(rows_left, masked, precision=highest, preferred_element_type=jnp....  9.03 us
    broadcast_in_dim x1, local copies, waits for them, and re-layouts, local(): jnp.repeat(jnp.repeat(tile_mask.astype(jnp.bfloat16), GENE_TILE, axis=0),...  8.96 us
  transfers between devices with their start and end apart: 2, of which 1 were waited for; matrix products, arithmetic and copies ran while one was open for 4% of the time, Pallas kernels for 0%

profile of v1, /device:TPU:1, one launch (start us, length us, event | category | flops | bytes accessed | tf_op | source)
XLA Modules:
  0.0 216.1 jit_solution(4451213346789194587)
XLA Ops:
  7.2 0.8 convert_element_type.7
  8.2 9.0 %broadcast_in_dim.16 = bf16[2048,16,128]{2,1,0:T(8,128)(2,1)S(1)} broadcast(bf16[2048,16]{1,0:T(8,128)(2,1)S(1)} %bitcast.68), dimensions={0,1} | broadcast | bytes 8454144 | tf_op jit(solution)/shard_map/broadcast_in_dim | solution.py:212
  17.1 3.2 %copy-done.4 = bf16[2048,16,128]{2,1,0:T(8,128)(2,1)} copy-done((bf16[2048,16,128]{2,1,0:T(8,128)(2,1)}, bf16[2048,16,128]{2,1,0:T(8,128)(2,1)S(1)}, u32[]{:S(2)}) %copy-start.4) | copy-done | bytes 8388632
  20.4 3.7 %fusion.15 = f32[2048,128]{1,0:T(8,128)} fusion(bf16[2048,128]{1,0:T(8,128)(2,1)S(1)} %copy-done, bf16[2048,2048]{1,0:T(8,128)(2,1)S(1)} %copy-done.5, bf16[256,8,16,128]{3,2,1,0:T(8,128)(2,1)S(1)} %bitcast.64), kind=kOutput, calls=%fused_computation.27 | convolution fusion | flops 1077936128 | bytes 18350080 | tf_op jit(solution)/shard_map/dot_general | solution.py:222
  24.1 7.4 %convolution_bitcast_fusion = f32[16,8,2048]{2,1,0:T(8,128)S(1)} fusion(f32[2048,128]{1,0:T(8,128)S(1)} %copy-done.1, bf16[2048,2048]{1,0:T(8,128)(2,1)} %param.5, bf16[256,8,16,128]{3,2,1,0:T(8,128)(2,1)} %bitcast.65), kind=kOutput, calls=%fused_computation.1 | convolution fusion | flops 1078198272 | bytes 18874368 | tf_op jit(solution)/shard_map/dot_general | solution.py:217
  31.5 24.3 %all_to_all.43 = f32[16,8,2048]{2,1,0:T(8,128)S(1)} all-to-all(f32[16,8,2048]{2,1,0:T(8,128)S(1)} %convolution_bitcast_fusion), channel_id=1, replica_groups=mesh['gene_0'=4,'gene_1'=4,'cell_0'=4,'cell_1'=2] {'gene_0','gene_1'}, dimensions={0} | all-to-all | bytes 2097152 | tf_op jit(solution)/shard_map/all_to_all | solution.py:25
  55.9 19.1 %all_to_all.44 = f32[16,8,2048]{2,1,0:T(8,128)S(1)} all-to-all(f32[16,8,2048]{2,1,0:T(8,128)S(1)} %broadcast_in_dim.17), channel_id=1, replica_groups=mesh['gene_0'=4,'gene_1'=4,'cell_0'=4,'cell_1'=2] {'gene_0','gene_1'}, dimensions={0} | all-to-all | bytes 2097152 | tf_op jit(solution)/shard_map/all_to_all | solution.py:38
  75.1 0.6 fusion.12
  75.7 16.0 %all-gather.1 = f32[1024,128]{1,0:T(8,128)S(1)} all-gather(f32[128,128]{1,0:T(8,128)S(1)} %fusion.12), channel_id=3, replica_groups=mesh['gene_0'=4,'gene_1'=4,'cell_0'=4,'cell_1'=2] {'cell_0','cell_1'}, dimensions={0}, use_global_device_ids=true | all-gather | bytes 589824 | tf_op jit(solution)/shard_map/all_gather | solution.py:60
  91.7 4.9 %reduce_sum.55 = f32[2048,128]{1,0:T(8,128)} reduce(f32[8,2048,128]{2,1,0:T(8,128)} %bitcast.63, f32[]{:T(128)} %constant.8.clone.1), dimensions={0}, to_apply=%region_1.0 | reduce | flops 1835008 | bytes 9437188 | tf_op jit(solution)/shard_map/reduce_sum | solution.py:60
  96.6 2.6 %copy.15 = f32[2048,128]{0,1:T(8,128)} copy(f32[2048,128]{1,0:T(8,128)} %reduce_sum.55) | data formatting | bytes 2097152 | tf_op jit(solution)/shard_map/reduce_sum | solution.py:60
  99.2 2.3 %fusion = f32[2048,128]{0,1:T(8,128)S(1)} fusion(f32[2048,128]{0,1:T(8,128)} %copy.15, f32[128,128]{1,0:T(8,128)S(1)} %reduce_sum.56, f32[2048,128]{1,0:T(8,128)S(1)} %copy-done.1), kind=kOutput, calls=%fused_computation.4 | convolution fusion | flops 402915328 | bytes 3211264 | tf_op jit(solution)/shard_map/dot_general | solution.py:225
  101.6 9.0 %fusion.14 = f32[128,2048]{1,0:T(8,128)S(1)} fusion(f32[2048,128]{0,1:T(8,128)S(1)} %fusion, bf16[2048,2048]{1,0:T(8,128)(2,1)} %param.5, bf16[256,8,16,128]{3,2,1,0:T(8,128)(2,1)} %bitcast.66), kind=kOutput, calls=%fused_computation.26 | convolution fusion | flops 6446645248 | bytes 18874368 | tf_op jit(solution)/shard_map/dot_general | solution.py:229
  110.6 1.2 fusion.16
  111.8 1.0 fusion.3
  112.8 1.1 copy.33
  114.0 4.3 %all-to-all-start.2 = ((f32[16,128,128]{2,1,0:T(8,128)}), f32[16,128,128]{2,1,0:T(8,128)}, u32[]{:S(2)}, u32[]{:S(2)}) async-start(f32[16,128,128]{2,1,0:T(8,128)} %bitcast.67), calls=%async_computation.2 | async-start | bytes 2097152 | tf_op jit(solution)/shard_map/all_to_all | solution.py:25
  118.4 18.2 %all-to-all-done.2 = f32[16,128,128]{2,1,0:T(8,128)} async-done(((f32[16,128,128]{2,1,0:T(8,128)}), f32[16,128,128]{2,1,0:T(8,128)}, u32[]{:S(2)}, u32[]{:S(2)}) %all-to-all-start.2) | async-done | bytes 1048608 | tf_op jit(solution)/shard_map/all_to_all | solution.py:25
  136.5 1.3 reduce_sum.57
  138.0 0.4 convolution_bitcast_fusion.4
  138.8 4.6 %all_to_all.45 = f32[2,64,640]{2,1,0:T(8,128)S(1)} all-to-all(f32[2,64,640]{2,1,0:T(8,128)S(1)} %copy.17), channel_id=1, replica_groups=mesh['gene_0'=4,'gene_1'=4,'cell_0'=4,'cell_1'=2] {'cell_1'}, dimensions={0} | all-to-all | bytes 655360 | tf_op jit(solution)/shard_map/all_to_all | solution.py:25
  143.6 14.2 %all_to_all.46 = f32[64,1,640]{2,1,0:T(1,128)S(1)} all-to-all(f32[64,1,640]{2,1,0:T(1,128)S(1)} %all_to_all.31), channel_id=1, replica_groups=mesh['gene_0'=4,'gene_1'=4,'cell_0'=4,'cell_1'=2] {'gene_0','gene_1','ce..., dimensions={0} | all-to-all | bytes 327680 | tf_op jit(solution)/shard_map/all_to_all | solution.py:66
  158.0 13.7 %all_to_all.47 = f32[64,1,640]{2,1,0:T(1,128)S(1)} all-to-all(f32[64,1,640]{2,1,0:T(1,128)S(1)} %broadcast_in_dim.18), channel_id=1, replica_groups=mesh['gene_0'=4,'gene_1'=4,'cell_0'=4,'cell_1'=2] {'gene_0','gene_1','ce..., dimensions={0} | all-to-all | bytes 327680 | tf_op jit(solution)/shard_map/all_to_all | solution.py:38
  171.8 6.6 %all_to_all.48 = f32[2,64,640]{2,1,0:T(8,128)S(1)} all-to-all(f32[2,64,640]{2,1,0:T(8,128)S(1)} %broadcast_in_dim.19), channel_id=1, replica_groups=mesh['gene_0'=4,'gene_1'=4,'cell_0'=4,'cell_1'=2] {'cell_1'}, dimensions={0} | all-to-all | bytes 655360 | tf_op jit(solution)/shard_map/all_to_all | solution.py:38
  178.9 1.0 slice.14
  179.9 0.7 slice.16.core_ref
  180.6 1.5 slice.17.gram_ref
  182.1 20.9 %subspace.1 = (f32[128,128]{1,0:T(8,128)}, f32[128,128]{1,0:T(8,128)}, f32[1,128]{1,0:T(1,128)}) custom-call(f32[256,256]{1,0:T(8,128)} %slice.16.core_ref, f32[128,128]{1,0:T(8,128)} %slice.17.gram_ref, f32[1,128]{1,0:T(1,128)} %bitcast.74), custom_call_target="tpu_custom_call" | custom-call | tf_op jit(solution)/shard_map/subspace/pallas_call | solution.py:192
  203.0 1.9 fusion.17
  204.9 1.9 fusion.2
  206.8 1.3 copy.21
  208.1 1.1 sqrt_bitcast_fusion
  (32 shorter events, 1.8 us)
Async XLA Ops:
  7.2 13.2 %copy-start = (bf16[2048,128]{1,0:T(8,128)(2,1)S(1)}, bf16[2048,128]{1,0:T(8,128)(2,1)}, u32[]{:S(2)}) copy-start(bf16[2048,128]{1,0:T(8,128)(2,1)} %param.8) | copy-start | bytes 1572868
  7.2 84.5 %all-gather.4.cloned.1.call-start = ((), (), s32[]{:S(2)}) async-start(), calls=%async_computation.7 | async-start | bytes 9437184 | tf_op jit(solution)/shard_map/all_gather | solution.py:60
  7.2 13.1 %copy-start.5 = (bf16[2048,2048]{1,0:T(8,128)(2,1)S(1)}, bf16[2048,2048]{1,0:T(8,128)(2,1)}, u32[]{:S(2)}) copy-start(bf16[2048,2048]{1,0:T(8,128)(2,1)} %param.5) | copy-start | bytes 25165828
  17.1 3.2 %copy-start.4 = (bf16[2048,16,128]{2,1,0:T(8,128)(2,1)}, bf16[2048,16,128]{2,1,0:T(8,128)(2,1)S(1)}, u32[]{:S(2)}) copy-start(bf16[2048,16,128]{2,1,0:T(8,128)(2,1)S(1)} %broadcast_in_dim.16) | copy-start | bytes 25165828
  20.4 3.7 %copy-start.1 = (f32[2048,128]{1,0:T(8,128)S(1)}, f32[2048,128]{1,0:T(8,128)}, u32[]{:S(2)}) copy-start(f32[2048,128]{1,0:T(8,128)} %param.6) | copy-start | bytes 3145732
  101.6 9.1 %copy-start.2 = (f32[2048,128]{0,1:T(8,128)}, f32[2048,128]{0,1:T(8,128)S(1)}, u32[]{:S(2)}) copy-start(f32[2048,128]{0,1:T(8,128)S(1)} %fusion) | copy-start | bytes 3145732
  114.0 22.6 %all-to-all-start.2 = ((f32[16,128,128]{2,1,0:T(8,128)}), f32[16,128,128]{2,1,0:T(8,128)}, u32[]{:S(2)}, u32[]{:S(2)}) async-start(f32[16,128,128]{2,1,0:T(8,128)} %bitcast.67), calls=%async_computation.2 | async-start | bytes 2097152 | tf_op jit(solution)/shard_map/all_to_all | solution.py:25
  118.4 84.6 %copy-start.3 = (f32[2048,128]{0,1:T(8,128)S(1)}, f32[2048,128]{0,1:T(8,128)}, u32[]{:S(2)}) copy-start(f32[2048,128]{0,1:T(8,128)} %copy-done.2) | copy-start | bytes 3145732
Sparse Core Ops, SparseCore 0:
  24.2 53.2 all-gather.3

commit v2 on v1

v2 whole, which is shorter than its diff:
```python
import functools
import jax
import jax.numpy as jnp
from jax import lax
from jax.experimental import pallas as pl
from jax.experimental.pallas import tpu as pltpu
from jax.sharding import Mesh
from jax.sharding import PartitionSpec as P

GENE_TILE = 256
CELL_TILE = 128
SWEEPS = 3
BLOCK = 32
CELL = ("cell_0", "cell_1")
GENE = ("gene_0", "gene_1")


AXES = (*GENE, *CELL)


def dot(left, right, left_dim, right_dim):
    return lax.dot_general(
        left,
        right,
        (((left_dim,), (right_dim,)), ((), ())),
        precision=lax.Precision.HIGHEST,
        preferred_element_type=jnp.float32,
    )


def identity(size):
    row = lax.broadcasted_iota(jnp.int32, (size, size), 0)
    column = lax.broadcasted_iota(jnp.int32, (size, size), 1)
    return jnp.where(row == column, 1.0, 0.0).astype(jnp.float32)


def inverse_factor(work, gram):
    size = gram.shape[0]
    work[:, :size] = gram
    work[:, size:] = identity(size)
    row_of = lax.broadcasted_iota(jnp.int32, (BLOCK, size), 0)
    for start in range(0, size, BLOCK):
        panel = work[start : start + BLOCK, :]
        columns = [
            jnp.broadcast_to(panel[:, start + j : start + j + 1], (BLOCK, size))
            for j in range(BLOCK)
        ]
        halves = [panel[:, :size], panel[:, size:]]
        pivots = jnp.zeros((BLOCK, size), jnp.float32)
        for j in range(BLOCK):
            column = columns[j]
            spread = jnp.broadcast_to(column[j : j + 1], (BLOCK, size))
            inverse = 1.0 / spread
            pivots = jnp.where(row_of == j, spread, pivots)
            for k in range(j + 1, BLOCK):
                lead = jnp.broadcast_to(column[k : k + 1], (BLOCK, size))
                columns[k] = columns[k] - column * (lead * inverse)
            ratio = jnp.where(row_of > j, column * inverse, 0.0)
            halves = [h - ratio * jnp.broadcast_to(h[j : j + 1], (BLOCK, size)) for h in halves]
        scale = lax.rsqrt(pivots)
        panel = jnp.concatenate([h * scale for h in halves], axis=1)
        work[start : start + BLOCK, :] = panel
        if start + BLOCK < size:
            update = dot(panel[:, :size], panel, 0, 0)
            work[start + BLOCK :, :] = work[start + BLOCK :, :] - update[start + BLOCK :, :]
    return work[:, size:]


def group_kernel(
    genes_local,
    counts_ref, loadings_ref, test_ref, tile_ref,
    sketch_ref, core_ref, gram_ref,
    masked, narrow, wide, split, turned, y_part, y_pair, y_ring, y_full,
    q_part, q_cell, q_gene, q_full, p_send, p_recv, z_send, z_recv,
    t_recv, t_full, c_send, c_recv, c_cell, c_full,
    load_sem, pair_sem, ring_sem, full_sem, send_sem, recv_sem,
):
    z, x, y, k = (lax.axis_index(a) for a in AXES)
    gene, cell = z * 4 + x, y * 2 + k
    f32, bf16 = jnp.float32, jnp.bfloat16
    rows = genes_local // 8
    gene_steps = [(a, b) for a in range(4) for b in range(4)][1:]
    cell_steps = [(a, b) for a in range(4) for b in range(2)][1:]

    def gene_at(step):
        return lax.rem(z + step[0], 4), lax.rem(x + step[1], 4)

    def cell_at(step):
        return lax.rem(y + step[0], 4), lax.rem(k + step[1], 2)

    def gene_device(at):
        return {"gene_0": at[0], "gene_1": at[1]}

    def cell_device(at):
        return {"cell_0": at[0], "cell_1": at[1]}

    def copy(source, target, sent, arrived, device):
        return pltpu.make_async_remote_copy(
            src_ref=source, dst_ref=target, send_sem=sent, recv_sem=arrived,
            device_id=device, device_id_type=pl.DeviceIdType.MESH,
        )

    partner = {"cell_1": 1 - k}

    def sent(ref, sem):
        copy(ref, ref, sem, sem, partner).wait_send()

    def arrived(ref, sem):
        copy(ref, ref, sem, sem, partner).wait_recv()

    def to_genes(phase, piece, target):
        for step in gene_steps:
            at = gene_at(step)
            copy(piece(at[0] * 4 + at[1]), target, send_sem.at[phase], recv_sem.at[phase],
                 gene_device(at)).start()

    def to_cells(phase, piece, target):
        for step in cell_steps:
            at = cell_at(step)
            copy(piece(at[0] * 2 + at[1]), target, send_sem.at[phase], recv_sem.at[phase],
                 cell_device(at)).start()

    loads = [
        pltpu.make_async_copy(
            counts_ref.at[pl.ds(t * rows, rows)], masked.at[pl.ds(t * rows, rows)], load_sem.at[t]
        )
        for t in range(8)
    ]
    for load in loads:
        load.start()
    barrier = pltpu.get_barrier_semaphore()
    for step in gene_steps:
        pl.semaphore_signal(barrier, inc=1, device_id=gene_device(gene_at(step)),
                            device_id_type=pl.DeviceIdType.MESH)
    for step in cell_steps:
        pl.semaphore_signal(barrier, inc=1, device_id=cell_device(cell_at(step)),
                            device_id_type=pl.DeviceIdType.MESH)
    narrow[...] = loadings_ref[...].T.astype(bf16)
    pl.semaphore_wait(barrier, len(gene_steps) + len(cell_steps))

    for t in range(8):
        loads[t].wait()
        for c in range(tile_ref.shape[1]):
            at = (slice(t * rows, (t + 1) * rows), slice(c * CELL_TILE, (c + 1) * CELL_TILE))
            block = masked[at]
            masked[at] = jnp.where(tile_ref[t, c] != 0, block, jnp.zeros_like(block))
        y_part[t] = jnp.dot(masked[t * rows:(t + 1) * rows], test_ref[...], preferred_element_type=f32)
        if t % 2:
            copy(y_part.at[t - k], y_pair.at[t // 2], pair_sem.at[0, t // 2], pair_sem.at[1, t // 2],
                 partner).start()

    high = y_part[...].reshape(genes_local, 128)
    wide[:, :128] = high.astype(bf16)
    wide[:, 128:] = (high - wide[:, :128].astype(f32)).astype(bf16)
    both = jnp.dot(narrow[...], wide[...], preferred_element_type=f32)
    q_part[...] = (both[:, :128] + both[:, 128:]).reshape(8, 16, 128)
    to_cells(0, lambda at: q_part.at[at], q_cell.at[cell])
    q_cell[cell] = q_part[cell]

    for t in range(4):
        arrived(y_pair.at[t], pair_sem.at[1, t])
        y_pair[t] = y_pair[t] + y_part[2 * t + k]
    for step in (1, 3, 2):
        to = lax.rem(y + step, 4)
        copy(y_pair.at[to], y_ring.at[y], ring_sem.at[0, step], ring_sem.at[1, y], {"cell_0": to}).start()
    y_ring[y] = y_pair[y]

    def project(e, carry):
        pair = lax.rem(gene // 2 + e, 8)
        lanes = pl.ds(pl.multiple_of(pair * 256, 256), 256)
        part = jnp.dot(narrow[...], masked[:, lanes], preferred_element_type=f32)
        p_send[2 * pair] = part[:, :128]
        p_send[2 * pair + 1] = part[:, 128:]
        return carry

    lax.fori_loop(0, 8, project, 0)
    arrived(q_cell.at[pl.ds(0, 7)], recv_sem.at[0])
    q_gene[gene] = jnp.sum(q_cell[...], axis=0)
    to_genes(1, lambda at: q_gene.at[gene], q_gene.at[gene])
    to_genes(2, lambda at: p_send.at[at], p_recv.at[gene])
    p_recv[gene] = p_send[gene]

    for step in (1, 2, 3):
        source = lax.rem(y + step, 4)
        arrived(y_ring.at[source], ring_sem.at[1, source])
    y_full[cell] = jnp.sum(y_ring[...], axis=0)
    for step in (1, 3, 2):
        to = lax.rem(y + step, 4)
        copy(y_full.at[cell], y_full.at[cell], full_sem.at[0, step], full_sem.at[1, cell], {"cell_0": to}).start()
    copy(y_full.at[cell], y_full.at[cell], full_sem.at[0, 0], full_sem.at[1, cell], partner).start()

    arrived(q_gene.at[pl.ds(0, 15)], recv_sem.at[1])
    q_full[cell] = jnp.sum(q_gene[...], axis=0)
    to_cells(3, lambda at: q_full.at[cell], q_full.at[cell])
    arrived(q_full.at[pl.ds(0, 7)], recv_sem.at[3])
    sketch_ref[...] = dot(loadings_ref[...], q_full[...].reshape(128, 128), 1, 0)
    for step in (1, 3, 2):
        source = lax.rem(y + step, 4) * 2 + k
        arrived(y_full.at[source], full_sem.at[1, source])
        copy(y_full.at[source], y_full.at[source], full_sem.at[0, 3 + step], full_sem.at[1, source],
             partner).start()
    for step in (0, 1, 3, 2):
        source = lax.rem(y + step, 4) * 2 + 1 - k
        arrived(y_full.at[source], full_sem.at[1, source])

    sketch_ref[...] = y_full[...].reshape(genes_local, 128) - sketch_ref[...]
    turned[...] = sketch_ref[...].T
    split[:128] = turned[...].astype(bf16)
    split[128:] = (turned[...] - split[:128].astype(f32)).astype(bf16)
    own = turned[pl.ds(pl.multiple_of(16 * cell, 16), 16), :]
    t_recv[gene, :, :128] = dot(own, loadings_ref[...], 1, 0)
    t_recv[gene, :, 128:] = dot(own, sketch_ref[...], 1, 0)
    to_genes(4, lambda at: t_recv.at[gene], t_recv.at[gene])

    def inner(e, carry):
        pair = lax.rem(gene // 2 + e, 8)
        lanes = pl.ds(pl.multiple_of(pair * 256, 256), 256)
        part = jnp.dot(split[...], masked[:, lanes], preferred_element_type=f32)
        part = part[:128] + part[128:]
        z_send[2 * pair] = part[:, :128]
        z_send[2 * pair + 1] = part[:, 128:]
        return carry

    def send_inner(at):
        copy(z_send.at[at], z_recv.at[gene], send_sem.at[5], recv_sem.at[5],
             {"gene_0": at // 4, "gene_1": lax.rem(at, 4)}).start()

    def inner_and_send(e, carry):
        inner(e, carry)
        pair = lax.rem(gene // 2 + e, 8)
        send_inner(2 * pair)
        send_inner(2 * pair + 1)
        return carry

    lax.fori_loop(1, 8, inner_and_send, 0)
    inner(0, 0)
    send_inner(gene + 1 - 2 * lax.rem(gene, 2))
    z_recv[gene] = z_send[gene]

    arrived(t_recv.at[pl.ds(0, 15)], recv_sem.at[4])
    t_full[cell] = jnp.sum(t_recv[...], axis=0)
    to_cells(6, lambda at: t_full.at[cell], t_full.at[cell])
    arrived(t_full.at[pl.ds(0, 7)], recv_sem.at[6])
    whole = t_full[...].reshape(128, 256)
    gram_ref[...] = whole[:, 128:]

    arrived(p_recv.at[pl.ds(0, 15)], recv_sem.at[2])
    projection = jnp.sum(p_recv[...], axis=0)
    arrived(z_recv.at[pl.ds(0, 15)], recv_sem.at[5])
    residual = jnp.sum(z_recv[...], axis=0) - dot(whole[:, :128], projection, 1, 0)
    c_send[:, :8] = dot(projection, projection, 1, 1).reshape(16, 8, 128)
    c_send[:, 8:16] = dot(residual, projection, 1, 1).reshape(16, 8, 128)
    c_send[:, 16:] = dot(residual, residual, 1, 1).reshape(16, 8, 128)
    to_genes(7, lambda at: c_send.at[at], c_recv.at[gene])
    c_recv[gene] = c_send[gene]
    arrived(c_recv.at[pl.ds(0, 15)], recv_sem.at[7])
    c_cell[cell] = jnp.sum(c_recv[...], axis=0)
    to_cells(8, lambda at: c_cell.at[cell], c_cell.at[cell])
    arrived(c_cell.at[pl.ds(0, 7)], recv_sem.at[8])
    c_full[gene] = jnp.sum(c_cell[...], axis=0)
    to_genes(9, lambda at: c_full.at[gene], c_full.at[gene])
    arrived(c_full.at[pl.ds(0, 15)], recv_sem.at[9])
    for part in range(3):
        core_ref[part] = c_full[:, 8 * part:8 * part + 8].reshape(128, 128)

    for t in range(4):
        sent(y_pair.at[t], pair_sem.at[0, t])
    for step in (1, 2, 3):
        sent(y_pair.at[0], ring_sem.at[0, step])
    for step in range(7):
        sent(y_full.at[0], full_sem.at[0, step])
    sent(q_cell.at[pl.ds(0, 7)], send_sem.at[0])
    sent(q_gene.at[pl.ds(0, 15)], send_sem.at[1])
    sent(p_recv.at[pl.ds(0, 15)], send_sem.at[2])
    sent(q_full.at[pl.ds(0, 7)], send_sem.at[3])
    sent(t_recv.at[pl.ds(0, 15)], send_sem.at[4])
    sent(z_recv.at[pl.ds(0, 15)], send_sem.at[5])
    sent(t_full.at[pl.ds(0, 7)], send_sem.at[6])
    sent(c_recv.at[pl.ds(0, 15)], send_sem.at[7])
    sent(c_cell.at[pl.ds(0, 7)], send_sem.at[8])
    sent(c_full.at[pl.ds(0, 15)], send_sem.at[9])


def group_call(counts, loadings, test_matrix, tile_mask):
    f32, bf16 = jnp.float32, jnp.bfloat16
    genes, cells = counts.shape
    whole = pl.BlockSpec(memory_space=pltpu.VMEM)
    dma = pltpu.SemaphoreType.DMA
    return pl.pallas_call(
        functools.partial(group_kernel, genes),
        out_shape=(
            jax.ShapeDtypeStruct((genes, 128), f32),
            jax.ShapeDtypeStruct((3, 128, 128), f32),
            jax.ShapeDtypeStruct((128, 128), f32),
        ),
        in_specs=[
            pl.BlockSpec(memory_space=pltpu.HBM),
            whole,
            whole,
            pl.BlockSpec(memory_space=pltpu.SMEM),
        ],
        out_specs=(whole, whole, whole),
        scratch_shapes=[
            pltpu.VMEM((genes, cells), bf16),
            pltpu.VMEM((128, genes), bf16),
            pltpu.VMEM((genes, 256), bf16),
            pltpu.VMEM((256, genes), bf16),
            pltpu.VMEM((128, genes), f32),
            pltpu.VMEM((8, genes // 8, 128), f32),
            pltpu.VMEM((4, genes // 8, 128), f32),
            pltpu.VMEM((4, genes // 8, 128), f32),
            pltpu.VMEM((8, genes // 8, 128), f32),
            pltpu.VMEM((8, 16, 128), f32),
            pltpu.VMEM((8, 16, 128), f32),
            pltpu.VMEM((16, 16, 128), f32),
            pltpu.VMEM((8, 16, 128), f32),
            pltpu.VMEM((16, 128, cells // 16), f32),
            pltpu.VMEM((16, 128, cells // 16), f32),
            pltpu.VMEM((16, 128, cells // 16), f32),
            pltpu.VMEM((16, 128, cells // 16), f32),
            pltpu.VMEM((16, 16, 256), f32),
            pltpu.VMEM((8, 16, 256), f32),
            pltpu.VMEM((16, 24, 128), f32),
            pltpu.VMEM((16, 24, 128), f32),
            pltpu.VMEM((8, 24, 128), f32),
            pltpu.VMEM((16, 24, 128), f32),
            dma((8,)),
            dma((2, 4)),
            dma((2, 4)),
            dma((2, 8)),
            dma((10,)),
            dma((10,)),
        ],
        compiler_params=pltpu.CompilerParams(
            collective_id=0, has_side_effects=True, vmem_limit_bytes=60 * 1024 * 1024
        ),
        name="group",
    )(counts, loadings, test_matrix, tile_mask)


def subspace_kernel(
    cells_total, genes_total, core_ref, gram_ref, values_ref, loadings_ref, sketch_ref,
    out_ref, squares_ref, work, core, subspace, basis,
):
    size = gram_ref.shape[0]
    basis[...] = inverse_factor(work, gram_ref[...])
    inverse = basis[...]
    values = values_ref[...]
    cross = dot(inverse, core_ref[1], 1, 0) / cells_total
    corner = dot(dot(inverse, core_ref[2], 1, 0), inverse, 1, 1)
    squares = jnp.broadcast_to(values * values, (size, size)) * identity(size)
    core[:size, :size] = core_ref[0] / cells_total + squares
    core[size:, :size] = cross
    core[:size, size:] = cross.T
    core[size:, size:] = corner / cells_total
    subspace[:size] = identity(size)
    subspace[size:] = jnp.zeros((size, size), jnp.float32)

    def sweep(step, carry):
        image = dot(core[...], subspace[...], 1, 0)
        rotation = inverse_factor(work, dot(image, image, 0, 0))
        subspace[...] = dot(image, rotation, 1, 1)
        return carry

    lax.fori_loop(0, SWEEPS, sweep, 0)
    final = dot(core[...], subspace[...], 1, 0)
    squares_ref[...] = jnp.sum(subspace[...] * final, axis=0, keepdims=True)
    top = subspace[:size]
    bottom = dot(basis[...], subspace[size:], 0, 0)
    rotated = dot(loadings_ref[...], top, 1, 0) + dot(sketch_ref[...], bottom, 1, 0)
    out_ref[...] = rotated * genes_total**0.5


def subspace_call(core, gram, values, loadings, sketch, cells_total, genes_total):
    size = gram.shape[0]
    return pl.pallas_call(
        functools.partial(subspace_kernel, cells_total, genes_total),
        out_shape=(
            jax.ShapeDtypeStruct(loadings.shape, jnp.float32),
            jax.ShapeDtypeStruct((1, size), jnp.float32),
        ),
        scratch_shapes=[
            pltpu.VMEM((size, 2 * size), jnp.float32),
            pltpu.VMEM((2 * size, 2 * size), jnp.float32),
            pltpu.VMEM((2 * size, size), jnp.float32),
            pltpu.VMEM((size, size), jnp.float32),
        ],
        name="subspace",
    )(core, gram, values.reshape(1, size), loadings, sketch)


def local(counts, loadings, values, test_matrix, tile_mask):
    cells_total = counts.shape[1] * lax.axis_size(CELL)
    genes_total = counts.shape[0] * lax.axis_size(GENE)
    sketch, core, gram = group_call(counts, loadings, test_matrix, tile_mask)
    new_loadings, squares = subspace_call(
        core, gram, values, loadings, sketch, cells_total, genes_total
    )
    return (new_loadings, jnp.sqrt(squares[0]))


def solution(mesh):
    torus = Mesh(mesh.devices.reshape(4, 4, 4, 2), ("gene_0", "gene_1", "cell_0", "cell_1"))
    placed = (P(GENE, CELL), P(GENE, None), P(), P(CELL, None), P(GENE, CELL))
    return jax.shard_map(
        local, mesh=torus, in_specs=placed, out_specs=(P(GENE, None), P()), check_vma=False
    )
```

time: 217 us -> 99.3 us (0.46)
  blocking collectives: 98.6 us -> 0 us
  Pallas kernels: 20.9 us -> 97.3 us
  matrix products: 29.7 us -> 0 us
  local copies, waits for them, and re-layouts: 22.8 us -> 1.18 us
  waiting for transfers between devices: 18.2 us -> 0 us
  between operations: 14.3 us -> 0.64 us
  other arithmetic: 7.25 us -> 0 us
  starting transfers between devices: 4.37 us -> 0 us
    all_to_all x6 -> x0, blocking collectives: 82.6 us -> none  [the longest x3 39.5 us: copy_for_each(): return lax.all_to_all(copies, axis, split_axis=0, concat_axis=0, tiled=True)]
    pallas_call x1 -> x2, Pallas kernels: 20.9 us -> 97.3 us  [the longest x1 73.4 us: group_call(): pl.pallas_call(functools.partial(group_kernel, genes), out_shape=(jax.Sha...]
    dot_general x11 -> x0, matrix products: 29.7 us -> none  [the longest x1 9.03 us: local(): jnp.dot(rows_left, masked, precision=highest, preferred_element_type=jnp....]
    all_to_all x1 -> x0, waiting for transfers between devices: 18.2 us -> none  [sent_and_summed(): lax.all_to_all(in_blocks(array, dim, length), axis, 0, 0, tiled=True)]
    all_gather x1 -> x0, blocking collectives: 16 us -> none  [total_of_pieces(): return lax.all_gather(array, axis).sum(0)]
    broadcast_in_dim x5 -> x0, local copies, waits for them, and re-layouts: 9.24 us -> none  [the longest x1 8.96 us: local(): jnp.repeat(jnp.repeat(tile_mask.astype(jnp.bfloat16), GENE_TILE, axis=0),...]
    reduce_sum x6 -> x0, other arithmetic: 6.39 us -> none  [the longest x2 4.9 us: total_of_pieces(): return lax.all_gather(array, axis).sum(0)]
    unnamed x15 -> x0, local copies, waits for them, and re-layouts: 4.7 us -> none
  transfers between devices with their start and end apart: 2 -> 0, of which waited for: 1 -> 0; matrix products, arithmetic and copies ran while one was open for 4% -> 0% of each run, Pallas kernels for 0% -> 0%
where the time goes in v2:
time: 99.3 us; the launch traced here: 99.1 us
  Pallas kernels  97.3 us (98%)
  local copies, waits for them, and re-layouts  1.18 us (1%)
    pallas_call x1, Pallas kernels, group_call(): pl.pallas_call(functools.partial(group_kernel, genes), out_shape=(jax.Sha...  73.4 us
    pallas_call x1, Pallas kernels, subspace_call(): pl.pallas_call(functools.partial(subspace_kernel, cells_total, genes_tota...  23.9 us

profile of v2, /device:TPU:1, one launch (start us, length us, event | category | flops | bytes accessed | tf_op | source)
XLA Modules:
  0.0 99.1 jit_solution(14547664548459573014)
XLA Ops:
  0.6 73.4 %group.1 = (f32[2048,128]{1,0:T(8,128)}, f32[3,128,128]{2,1,0:T(8,128)}, f32[128,128]{1,0:T(8,128)}) custom-call(bf16[2048,2048]{1,0:T(8,128)(2,1)} %counts_ref.1, f32[2048,128]{1,0:T(8,128)} %loadings_ref.3, bf16[2048,128]{1,0:T(8,128)(2,1)} %test_ref.1, s32[8,16]{1,0:T(8,128)} %tile_ref.1), custom_call_target="tpu_custom_call" | custom-call | tf_op jit(solution)/shard_map/group/pallas_call | solution.py:289
  74.0 23.9 %subspace.1 = (f32[2048,128]{1,0:T(8,128)}, f32[1,128]{1,0:T(1,128)}) custom-call(f32[3,128,128]{2,1,0:T(8,128)} %get-tuple-element.7.core_ref, f32[128,128]{1,0:T(8,128)} %get-tuple-element.8.gram_ref, f32[1,128]{1,0:T(1,128)} %bitcast.3, f32[2048,128]{1,0:T(8,128)} %loadings_ref.3, f32[2048,128]{1,0:T(8,128)} %get-tuple-element.9.sketch_ref), custom_call_target="tpu_custom_call" | custom-call | tf_op jit(solution)/shard_map/subspace/pallas_call | solution.py:376
  97.9 1.2 %sqrt_bitcast_fusion = f32[128]{0:T(128)} fusion(f32[1,128]{1,0:T(1,128)} %get-tuple-element.11), kind=kLoop, calls=%fused_computation | loop fusion | bytes 1024 | tf_op jit(solution)/shard_map/sqrt | solution.py:399

commit v3 on v2

v3 whole, which is shorter than its diff:
```python
import functools
import jax
import jax.numpy as jnp
from jax import lax
from jax.experimental import pallas as pl
from jax.experimental.pallas import tpu as pltpu
from jax.sharding import Mesh
from jax.sharding import PartitionSpec as P

GENE_TILE = 256
CELL_TILE = 128
SWEEPS = 3
BLOCK = 32
COLUMNS = 16
GROUP_VMEM = 52 * 1024 * 1024
CELL = ("cell_0", "cell_1")
GENE = ("gene_0", "gene_1")


AXES = (*GENE, *CELL)


def dot(left, right, left_dim, right_dim):
    return lax.dot_general(
        left,
        right,
        (((left_dim,), (right_dim,)), ((), ())),
        precision=lax.Precision.HIGHEST,
        preferred_element_type=jnp.float32,
    )


def identity(size):
    row = lax.broadcasted_iota(jnp.int32, (size, size), 0)
    column = lax.broadcasted_iota(jnp.int32, (size, size), 1)
    return jnp.where(row == column, 1.0, 0.0).astype(jnp.float32)


def three_parts(array):
    first = array.astype(jnp.bfloat16)
    rest = array - first.astype(jnp.float32)
    second = rest.astype(jnp.bfloat16)
    return first, second, (rest - second.astype(jnp.float32)).astype(jnp.bfloat16)


def left_parts(array, dim):
    a, b, c = three_parts(array)
    return jnp.concatenate([a, a, b, a, b, c], axis=dim)


def right_parts(array, dim):
    a, b, c = three_parts(array)
    return jnp.concatenate([a, b, a, c, b, a], axis=dim)


def of_parts(left, right, left_dim=1):
    return lax.dot_general(
        left, right, (((left_dim,), (0,)), ((), ())), preferred_element_type=jnp.float32
    )


def inverse_factor(work, gram):
    size = gram.shape[0]
    groups = range(BLOCK // 8)
    work[:, :size] = gram
    work[:, size:] = identity(size)
    row_of = lax.broadcasted_iota(jnp.int32, (8, size), 0)

    def spread(rows, at):
        return jnp.broadcast_to(rows[at : at + 1], (8, size))

    for start in range(0, size, BLOCK):
        halves = [
            [work[start + 8 * g : start + 8 * g + 8, h : h + size] for g in groups]
            for h in (0, size)
        ]
        pivots = [jnp.zeros((8, size), jnp.float32) for g in groups]
        for j in range(BLOCK):
            own, at = j // 8, j % 8
            if j % COLUMNS == 0:
                columns = {
                    k: {
                        g: jnp.broadcast_to(halves[0][g][:, start + k : start + k + 1], (8, size))
                        for g in groups[k // 8 :]
                    }
                    for k in range(j, j + COLUMNS)
                }
                pivot = spread(columns[j][own], at)
                inverse = 1.0 / pivot
            pivots[own] = jnp.where(row_of == at, pivot, pivots[own])
            ratios = {g: c * inverse for g, c in columns[j].items()}
            others = range(j + 1, j - j % COLUMNS + COLUMNS)
            if others:
                after, below = (j + 1) // 8, (j + 1) % 8
                edge = spread(columns[j][after], below)
                first = edge * inverse
                pivot = spread(columns[j + 1][after], below) - edge * first
                inverse = 1.0 / pivot
            for k in others:
                lead = first if k == j + 1 else spread(ratios[k // 8], k % 8)
                for g in groups[k // 8 :]:
                    columns[k][g] = columns[k][g] - columns[j][g] * lead
            ratios[own] = jnp.where(row_of > at, ratios[own], 0.0)
            for half in halves:
                top = spread(half[own], at)
                for g in groups[own:]:
                    half[g] = half[g] - ratios[g] * top
        scales = [lax.rsqrt(pivot) for pivot in pivots]
        panel = jnp.concatenate(
            [jnp.concatenate([half[g] * scales[g] for g in groups], axis=0) for half in halves],
            axis=1,
        )
        work[start : start + BLOCK, :] = panel
        if start + BLOCK < size:
            update = of_parts(left_parts(panel[:, :size], 0), right_parts(panel, 0), 0)
            work[start + BLOCK :, :] = work[start + BLOCK :, :] - update[start + BLOCK :, :]
    return work[:, size:]


def group_kernel(
    genes_local, cells_total, genes_total,
    counts_ref, loadings_hbm, test_ref, tile_ref, values_ref,
    out_ref, singular_ref,
    loadings_ref, high_ref, low_ref, core, basis_ref, image,
    masked, narrow, wide, split, fitted, work, y_part, y_pair, y_ring, y_full,
    q_part, q_cell, q_gene, q_full, p_send, p_one, p_mid, p_two, z_send, z_one, z_mid, z_two,
    t_one, t_two, t_full, c_send, c_recv, c_cell, c_full,
    load_sem, pair_sem, ring_sem, full_sem, send_sem, recv_sem,
):
    z, x, y, k = (lax.axis_index(a) for a in AXES)
    gene, cell = z * 4 + x, y * 2 + k
    near, far = z + k * (x - z), x + k * (z - x)
    f32, bf16 = jnp.float32, jnp.bfloat16
    rows = genes_local // 8
    gene_steps = [(m, n) for m in range(4) for n in range(4)][1:]
    cell_steps = [(m, n) for m in range(4) for n in range(2)][1:]

    def gene_at(step):
        return lax.rem(z + step[0], 4), lax.rem(x + step[1], 4)

    def cell_at(step):
        return lax.rem(y + step[0], 4), lax.rem(k + step[1], 2)

    def gene_device(at):
        return {"gene_0": at[0], "gene_1": at[1]}

    def cell_device(at):
        return {"cell_0": at[0], "cell_1": at[1]}

    def line_device(first, second):
        return gene_device((first + k * (second - first), second + k * (first - second)))

    def copy(source, target, sent, arrived, device):
        return pltpu.make_async_remote_copy(
            src_ref=source, dst_ref=target, send_sem=sent, recv_sem=arrived,
            device_id=device, device_id_type=pl.DeviceIdType.MESH,
        )

    partner = {"cell_1": 1 - k}

    def sent(ref, sem):
        copy(ref, ref, sem, sem, partner).wait_send()

    def arrived(ref, sem):
        copy(ref, ref, sem, sem, partner).wait_recv()

    def to_genes(phase, piece, target):
        for step in gene_steps:
            at = gene_at(step)
            copy(piece(at[0] * 4 + at[1]), target, send_sem.at[phase], recv_sem.at[phase],
                 gene_device(at)).start()

    def to_cells(phase, piece, target):
        for step in cell_steps:
            at = cell_at(step)
            copy(piece(at[0] * 2 + at[1]), target, send_sem.at[phase], recv_sem.at[phase],
                 cell_device(at)).start()

    def to_near(phase, at, source, target):
        copy(source, target, send_sem.at[phase], recv_sem.at[phase], line_device(at, far)).start()

    def to_far(phase, at, source, target):
        copy(source, target, send_sem.at[phase], recv_sem.at[phase], line_device(near, at)).start()

    def three(ref):
        return ref.at[pl.ds(0, 3)]

    order = [lax.rem(y + step, 4) for step in (2, 1, 3, 0)]
    tiles = [2 * at + lax.rem(k + turn, 2) for at in order for turn in (1, 0)]

    def load(t):
        at = pl.ds(pl.multiple_of(t * rows, rows), rows)
        return pltpu.make_async_copy(counts_ref.at[at], masked.at[at], load_sem.at[t])

    loadings_copy = pltpu.make_async_copy(loadings_hbm, loadings_ref, load_sem.at[8])
    for t in tiles[:2]:
        load(t).start()
    loadings_copy.start()
    for t in tiles[2:]:
        load(t).start()
    barrier = pltpu.get_barrier_semaphore()
    for step in gene_steps:
        pl.semaphore_signal(barrier, inc=1, device_id=gene_device(gene_at(step)),
                            device_id_type=pl.DeviceIdType.MESH)
    for step in cell_steps:
        pl.semaphore_signal(barrier, inc=1, device_id=cell_device(cell_at(step)),
                            device_id_type=pl.DeviceIdType.MESH)
    def sketch_rows(t):
        load(t).wait()
        at = pl.ds(pl.multiple_of(t * rows, rows), rows)
        for c in range(tile_ref.shape[1]):
            lanes = slice(c * CELL_TILE, (c + 1) * CELL_TILE)
            block = masked[at, lanes]
            masked[at, lanes] = jnp.where(tile_ref[t, c] != 0, block, jnp.zeros_like(block))
        y_part[t] = jnp.dot(masked[at], test_ref[...], preferred_element_type=f32)

    def pair_sum(n):
        arrived(y_pair.at[order[n]], pair_sem.at[1, order[n]])
        y_pair[order[n]] = y_pair[order[n]] + y_part[2 * order[n] + k]

    def send_along(n):
        pair_sum(n)
        copy(y_pair.at[order[n]], y_ring.at[y], ring_sem.at[0, n], ring_sem.at[1, y],
             {"cell_0": order[n]}).start()

    sketch_rows(tiles[0])
    loadings_copy.wait()
    high_ref[:, :128] = loadings_ref[...].astype(bf16)
    narrow[...] = high_ref[:, :128].T
    pl.semaphore_wait(barrier, len(gene_steps) + len(cell_steps))
    for n in range(4):
        if n:
            sketch_rows(tiles[2 * n])
        copy(y_part.at[tiles[2 * n]], y_pair.at[order[n]], pair_sem.at[0, n],
             pair_sem.at[1, order[n]], partner).start()
        sketch_rows(tiles[2 * n + 1])
        if n:
            send_along(n - 1)

    whole = y_part[...].reshape(genes_local, 128)
    wide[:, :128] = whole.astype(bf16)
    wide[:, 128:] = (whole - wide[:, :128].astype(f32)).astype(bf16)
    both = jnp.dot(narrow[...], wide[...], preferred_element_type=f32)
    q_part[...] = (both[:, :128] + both[:, 128:]).reshape(16, 8, 128)
    to_genes(0, lambda at: q_part.at[at], q_gene.at[gene])
    q_gene[gene] = q_part[gene]
    pair_sum(3)
    y_ring[y] = y_pair[y]

    def lanes_of(at):
        return pl.ds(pl.multiple_of(at * 512, 512), 512)

    def project(step, carry):
        at = lax.rem(near + step, 4)
        part = jnp.dot(narrow[...], masked[:, lanes_of(at)], preferred_element_type=f32)
        for n in range(4):
            p_send[at, n] = part[:, 128 * n:128 * n + 128]
        return carry

    lax.fori_loop(0, 4, project, 0)
    for step in (2, 1, 3):
        at = lax.rem(near + step, 4)
        to_near(2, at, p_send.at[at], p_one.at[near])
    p_one[near] = p_send[near]

    low_ref[:, :128] = (loadings_ref[...] - high_ref[:, :128].astype(f32)).astype(bf16)
    arrived(q_gene.at[pl.ds(0, 15)], recv_sem.at[0])
    q_cell[cell] = jnp.sum(q_gene[...], axis=0)
    to_cells(1, lambda at: q_cell.at[cell], q_cell.at[cell])
    for step in (1, 3, 2):
        source = lax.rem(y + step, 4)
        arrived(y_ring.at[source], ring_sem.at[1, source])
    y_full[cell] = jnp.sum(y_ring[...], axis=0)
    for n, step in enumerate((2, 1, 3)):
        to = lax.rem(y + step, 4)
        copy(y_full.at[cell], y_full.at[cell], full_sem.at[0, 1 + n], full_sem.at[1, cell],
             {"cell_0": to}).start()
    copy(y_full.at[cell], y_full.at[cell], full_sem.at[0, 0], full_sem.at[1, cell], partner).start()
    arrived(q_cell.at[pl.ds(0, 7)], recv_sem.at[1])
    q_full[gene] = jnp.sum(q_cell[...], axis=0)
    to_genes(3, lambda at: q_full.at[gene], q_full.at[gene])
    arrived(three(p_one), recv_sem.at[2])
    p_mid[...] = jnp.sum(p_one[...], axis=0)
    for step in (2, 1, 3):
        at = lax.rem(far + step, 4)
        to_far(6, at, p_mid.at[at], p_two.at[far])
    p_two[far] = p_mid[far]

    arrived(q_full.at[pl.ds(0, 15)], recv_sem.at[3])
    fitted[...] = dot(loadings_ref[...], q_full[...].reshape(128, 128), 1, 0).reshape(8, rows, 128)

    def sketch_part(source):
        at = pl.ds(pl.multiple_of(source * rows, rows), rows)
        part = y_full[source] - fitted[source]
        upper = part.astype(bf16)
        lower = (part - upper.astype(f32)).astype(bf16)
        high_ref[at, 128:] = upper
        low_ref[at, 128:] = lower
        split[:128, at] = upper.T
        split[128:, at] = lower.T

    def arrive_and_split(source):
        arrived(y_full.at[source], full_sem.at[1, source])
        sketch_part(source)

    sketch_part(cell)
    arrive_and_split(2 * y + 1 - k)
    for step in (1, 3, 2):
        source = lax.rem(y + step, 4) * 2 + k
        arrived(y_full.at[source], full_sem.at[1, source])
        copy(y_full.at[source], y_full.at[source], full_sem.at[0, 3 + step],
             full_sem.at[1, source], partner).start()
        sketch_part(source)
    for step in (1, 3, 2):
        arrive_and_split(lax.rem(y + step, 4) * 2 + 1 - k)


    own = jnp.concatenate(
        [split[pl.ds(pl.multiple_of(16 * cell + h, 16), 16), :] for h in (0, 128)], axis=0
    )
    part = jnp.dot(own, high_ref[...], preferred_element_type=f32)
    part = part + jnp.dot(own, low_ref[...], preferred_element_type=f32)
    t_one[near] = part[:16] + part[16:]
    for step in (2, 1, 3):
        to_near(4, lax.rem(near + step, 4), t_one.at[near], t_one.at[near])

    def inner(at, half):
        lanes = pl.ds(pl.multiple_of(at * 512 + half * 256, 256), 256)
        part = jnp.dot(split[...], masked[:, lanes], preferred_element_type=f32)
        part = part[:128] + part[128:]
        for n in range(2):
            z_send[at, 2 * half + n] = part[:, 128 * n:128 * n + 128]

    for step in (2, 1, 3):
        at = lax.rem(near + step, 4)
        for half in range(2):
            inner(at, half)
            to_near(5, at, z_send.at[at, pl.ds(2 * half, 2)], z_one.at[near, pl.ds(2 * half, 2)])
    arrived(three(t_one), recv_sem.at[4])
    t_two[far] = jnp.sum(t_one[...], axis=0)
    for step in (2, 1, 3):
        to_far(7, lax.rem(far + step, 4), t_two.at[far], t_two.at[far])
    inner(near, 0)
    inner(near, 1)
    z_one[near] = z_send[near]
    arrived(three(t_two), recv_sem.at[7])
    t_full[cell] = jnp.sum(t_two[...], axis=0)
    to_cells(8, lambda at: t_full.at[cell], t_full.at[cell])
    arrived(three(z_one), recv_sem.at[5])
    for step in (2, 1, 3):
        at = lax.rem(far + step, 4)
        z_mid[at] = jnp.sum(z_one[:, at], axis=0)
        to_far(9, at, z_mid.at[at], z_two.at[far])
    z_two[far] = jnp.sum(z_one[:, far], axis=0)
    arrived(t_full.at[pl.ds(0, 7)], recv_sem.at[8])

    arrived(three(p_two), recv_sem.at[6])
    projection = jnp.sum(p_two[...], axis=0)
    explained = dot(t_full[...].reshape(128, 256)[:, :128], projection, 1, 0)
    c_send[:, :8] = dot(projection, projection, 1, 1).reshape(16, 8, 128)
    arrived(three(z_two), recv_sem.at[9])
    residual = jnp.sum(z_two[...], axis=0) - explained
    c_send[:, 8:16] = dot(residual, projection, 1, 1).reshape(16, 8, 128)
    c_send[:, 16:] = dot(residual, residual, 1, 1).reshape(16, 8, 128)
    to_genes(10, lambda at: c_send.at[at], c_recv.at[gene])
    c_recv[gene] = c_send[gene]
    products = t_full[...].reshape(128, 256)
    basis_ref[...] = inverse_factor(work, products[:, 128:])
    arrived(c_recv.at[pl.ds(0, 15)], recv_sem.at[10])
    c_cell[cell] = jnp.sum(c_recv[...], axis=0)
    to_cells(11, lambda at: c_cell.at[cell], c_cell.at[cell])
    arrived(c_cell.at[pl.ds(0, 7)], recv_sem.at[11])
    c_full[gene] = jnp.sum(c_cell[...], axis=0)
    to_genes(12, lambda at: c_full.at[gene], c_full.at[gene])
    arrived(c_full.at[pl.ds(0, 15)], recv_sem.at[12])
    parts = [c_full[:, 8 * n:8 * n + 8].reshape(128, 128) for n in range(3)]
    size = 128
    inverse = basis_ref[...]
    values = values_ref[...]
    mixed = dot(inverse, jnp.concatenate(parts[1:], axis=1), 1, 0)
    cross = mixed[:, :size] / cells_total
    corner = dot(mixed[:, size:], inverse, 1, 1)
    squares = jnp.broadcast_to(values * values, (size, size)) * identity(size)
    image[:, :size] = parts[0] / cells_total + squares
    image[:, size:] = cross.T
    core[...] = right_parts(
        jnp.concatenate(
            [image[...], jnp.concatenate([cross, corner / cells_total], axis=1)], axis=0
        ),
        0,
    )

    def rotation_of(last):
        return left_parts(inverse_factor(work, dot(last, last, 1, 1)), 1)

    def sweep(step, carry):
        last = image[...]
        following = right_parts(of_parts(left_parts(last, 1), core[...]), 0)
        image[...] = of_parts(rotation_of(last), following)
        return carry

    lax.fori_loop(0, SWEEPS - 1, sweep, 0)
    last = image[...]
    following = right_parts(of_parts(left_parts(last, 1), core[...]), 0)
    lifted = of_parts(left_parts(last[:, size:], 1), right_parts(basis_ref[...], 0))
    lifted = right_parts(jnp.concatenate([last[:, :size], lifted], axis=1), 0)
    last_parts = right_parts(last, 0)
    rotation = rotation_of(last)
    turn = of_parts(rotation, lifted) * genes_total**0.5
    upper = turn.astype(jnp.bfloat16)
    lower = (turn - upper.astype(jnp.float32)).astype(jnp.bfloat16)
    turns = jnp.concatenate([upper, lower], axis=0)

    def onto(left, right):
        return lax.dot_general(
            left, right, (((1,), (1,)), ((), ())), preferred_element_type=jnp.float32
        )

    both = onto(high_ref[...], turns)
    out_ref[...] = both[:, :size] + (both[:, size:] + onto(low_ref[...], upper))
    products = of_parts(rotation, last_parts) * of_parts(rotation, following)
    singular_ref[...] = jnp.sqrt(jnp.sum(products.T, axis=0, keepdims=True))

    for n in range(4):
        sent(y_pair.at[0], pair_sem.at[0, n])
    for n in range(3):
        sent(y_pair.at[0], ring_sem.at[0, n])
    for n in range(7):
        sent(y_full.at[0], full_sem.at[0, n])
    for phase, ref in ((1, q_cell), (8, t_full), (11, c_cell)):
        sent(ref.at[pl.ds(0, 7)], send_sem.at[phase])
    for phase, ref in ((0, q_gene), (3, q_full), (10, c_recv), (12, c_full)):
        sent(ref.at[pl.ds(0, 15)], send_sem.at[phase])
    for phase, ref in ((2, p_one), (4, t_one), (5, z_one), (6, p_two), (7, t_two), (9, z_two)):
        sent(three(ref), send_sem.at[phase])


def group_call(counts, loadings, test_matrix, tile_mask, values, cells_total, genes_total):
    f32, bf16 = jnp.float32, jnp.bfloat16
    genes, cells = counts.shape
    rows, share = genes // 8, cells // 16
    whole = pl.BlockSpec(memory_space=pltpu.VMEM)
    dma = pltpu.SemaphoreType.DMA
    quarter = pltpu.VMEM((4, 4, 128, share), f32)
    return pl.pallas_call(
        functools.partial(group_kernel, genes, cells_total, genes_total),
        out_shape=(
            jax.ShapeDtypeStruct((genes, 128), f32),
            jax.ShapeDtypeStruct((1, 128), f32),
        ),
        in_specs=[
            pl.BlockSpec(memory_space=pltpu.HBM),
            pl.BlockSpec(memory_space=pltpu.HBM),
            whole,
            pl.BlockSpec(memory_space=pltpu.SMEM),
            whole,
        ],
        out_specs=(whole, whole),
        scratch_shapes=[
            pltpu.VMEM((genes, 128), f32),
            pltpu.VMEM((genes, 256), bf16),
            pltpu.VMEM((genes, 256), bf16),
            pltpu.VMEM((6 * 256, 256), bf16),
            pltpu.VMEM((128, 128), f32),
            pltpu.VMEM((128, 256), f32),
            pltpu.VMEM((genes, cells), bf16),
            pltpu.VMEM((128, genes), bf16),
            pltpu.VMEM((genes, 256), bf16),
            pltpu.VMEM((256, genes), bf16),
            pltpu.VMEM((8, rows, 128), f32),
            pltpu.VMEM((128, 256), f32),
            pltpu.VMEM((8, rows, 128), f32),
            pltpu.VMEM((4, rows, 128), f32),
            pltpu.VMEM((4, rows, 128), f32),
            pltpu.VMEM((8, rows, 128), f32),
            pltpu.VMEM((16, 8, 128), f32),
            pltpu.VMEM((8, 8, 128), f32),
            pltpu.VMEM((16, 8, 128), f32),
            pltpu.VMEM((16, 8, 128), f32),
            quarter,
            quarter,
            pltpu.VMEM((4, 128, share), f32),
            pltpu.VMEM((4, 128, share), f32),
            quarter,
            quarter,
            pltpu.VMEM((4, 128, share), f32),
            pltpu.VMEM((4, 128, share), f32),
            pltpu.VMEM((4, 16, 256), f32),
            pltpu.VMEM((4, 16, 256), f32),
            pltpu.VMEM((8, 16, 256), f32),
            pltpu.VMEM((16, 24, 128), f32),
            pltpu.VMEM((16, 24, 128), f32),
            pltpu.VMEM((8, 24, 128), f32),
            pltpu.VMEM((16, 24, 128), f32),
            dma((9,)),
            dma((2, 4)),
            dma((2, 4)),
            dma((2, 8)),
            dma((13,)),
            dma((13,)),
        ],
        compiler_params=pltpu.CompilerParams(
            collective_id=0, has_side_effects=True, vmem_limit_bytes=GROUP_VMEM
        ),
        name="group",
    )(counts, loadings, test_matrix, tile_mask, values.reshape(1, -1))


def local(counts, loadings, values, test_matrix, tile_mask):
    cells_total = counts.shape[1] * lax.axis_size(CELL)
    genes_total = counts.shape[0] * lax.axis_size(GENE)
    new_loadings, singular = group_call(
        counts, loadings, test_matrix, tile_mask, values, cells_total, genes_total
    )
    return (new_loadings, singular[0])


def solution(mesh):
    torus = Mesh(mesh.devices.reshape(4, 4, 4, 2), ("gene_0", "gene_1", "cell_0", "cell_1"))
    placed = (P(GENE, CELL), P(GENE, None), P(), P(CELL, None), P(GENE, CELL))
    return jax.shard_map(
        local, mesh=torus, in_specs=placed, out_specs=(P(GENE, None), P()), check_vma=False
    )
```

time: 99.3 us -> 75.7 us (0.76)
  Pallas kernels: 97.3 us -> 70.8 us
  local copies, waits for them, and re-layouts: 1.18 us -> 3.86 us
    pallas_call x2 -> x1, Pallas kernels: 97.3 us -> 70.8 us  [group_call(): pl.pallas_call(functools.partial(group_kernel, genes, cells_total, genes_...]
    unnamed x0 -> x8, local copies, waits for them, and re-layouts: none -> 3.86 us
    sqrt x1 -> x0, local copies, waits for them, and re-layouts: 1.18 us -> none  [local(): return (new_loadings, jnp.sqrt(squares[0]))]
where the time goes in v3:
time: 75.7 us; the launch traced here: 75.4 us
  Pallas kernels  70.8 us (94%)
  local copies, waits for them, and re-layouts  3.86 us (5%)
    pallas_call x1, Pallas kernels, group_call(): pl.pallas_call(functools.partial(group_kernel, genes, cells_total, genes_...  70.8 us
    unnamed x8, local copies, waits for them, and re-layouts  3.86 us

profile of v3, /device:TPU:1, one launch (start us, length us, event | category | flops | bytes accessed | tf_op | source)
XLA Modules:
  0.0 75.4 jit_solution(13886995385610439420)
XLA Ops:
  0.6 0.0 copy-start
  0.6 1.0 %copy-done = bf16[2048,128]{1,0:T(8,128)(2,1)S(1)} copy-done((bf16[2048,128]{1,0:T(8,128)(2,1)S(1)}, bf16[2048,128]{1,0:T(8,128)(2,1)}, u32[]{:S(2)}) %copy-start) | copy-done | bytes 524312
  1.7 0.0 copy-start.1
  1.7 0.7 copy-done.1
  2.4 0.0 copy-start.2
  2.4 0.7 copy-done.2
  3.0 70.8 %group.1 = (f32[2048,128]{1,0:T(8,128)S(1)}, f32[1,128]{1,0:T(1,128)S(1)}) custom-call(bf16[2048,2048]{1,0:T(8,128)(2,1)} %counts_ref.1, f32[2048,128]{1,0:T(8,128)} %loadings_hbm.1, bf16[2048,128]{1,0:T(8,128)(2,1)S(1)} %copy-done, s32[8,16]{1,0:T(8,128)S(1)} %copy-done.1, f32[1,128]{1,0:T(1,128)S(1)} %bitcast.2), custom_call_target="tpu_custom_call" | custom-call | tf_op jit(solution)/shard_map/group/pallas_call | solution.py:445
  73.9 1.0 %copy.9 = f32[2048,128]{1,0:T(8,128)} copy(f32[2048,128]{1,0:T(8,128)S(1)} %get-tuple-element.8) | data formatting | bytes 2097152
  74.8 0.5 copy.10
Async XLA Ops:
  0.6 1.0 %copy-start = (bf16[2048,128]{1,0:T(8,128)(2,1)S(1)}, bf16[2048,128]{1,0:T(8,128)(2,1)}, u32[]{:S(2)}) copy-start(bf16[2048,128]{1,0:T(8,128)(2,1)} %test_ref.1) | copy-start | bytes 1572868
  1.7 0.7 copy-start.1
  2.4 0.7 copy-start.2
